TPU v7x, 32 devices: a whole 2x2x4 slice. The times are simulated.
32 devices in a mesh: dp: 16 (over z, y, x), seq: 2 (over core).
Axes of the slice: x: 2, y: 2, z: 4, core: 2. Of those that a mesh axis runs over, the one named last changes fastest.
Arguments:
- chains_in: bfloat16 [128, 160, 768], P(('dp', 'seq')), may hold values from -6 to 6
- lengths: int32 [128], P(('dp', 'seq')), may hold values from 95 to 160
- d_out: bfloat16 [128, 160, 768], P(('dp', 'seq')), may hold values from -6 to 6
- w_query: bfloat16 [768, 768], replicated, may hold values from -0.21875 to 0.21875
- b_query: float32 [768], replicated, may hold values from -3 to 3
- w_key: bfloat16 [768, 768], replicated, may hold values from -0.21875 to 0.21875
- w_value: bfloat16 [768, 768], replicated, may hold values from -0.21875 to 0.21875
- b_value: float32 [768], replicated, may hold values from -3 to 3
- w_output: bfloat16 [768, 768], replicated, may hold values from -2.5 to 2.5
- b_output: float32 [768], replicated, may hold values from -3 to 3
- gain_one: float32 [768], replicated, may hold values from 0.25 to 1.75
- shift_one: float32 [768], replicated, may hold values from -2 to 2
- w_inner: bfloat16 [768, 3072], replicated, may hold values from -0.21875 to 0.21875
- b_inner: float32 [3072], replicated, may hold values from -3 to 3
- w_outer: bfloat16 [3072, 768], replicated, may hold values from -0.109375 to 0.109375
- b_outer: float32 [768], replicated, may hold values from -3 to 3
- gain_two: float32 [768], replicated, may hold values from 0.25 to 1.75
- shift_two: float32 [768], replicated, may hold values from -2 to 2
Outputs:
- layer_out: bfloat16 [128, 160, 768], P(('dp', 'seq'))
- d_x: float32 [128, 160, 768], P(('dp', 'seq'))
- d_w_query: float32 [768, 768], replicated
- d_b_query: float32 [768], replicated
- d_w_key: float32 [768, 768], replicated
- d_w_value: float32 [768, 768], replicated
- d_b_value: float32 [768], replicated
- d_w_output: float32 [768, 768], replicated
- d_b_output: float32 [768], replicated
- d_gain_one: float32 [768], replicated
- d_shift_one: float32 [768], replicated
- d_w_inner: float32 [768, 3072], replicated
- d_b_inner: float32 [3072], replicated
- d_w_outer: float32 [3072, 768], replicated
- d_b_outer: float32 [768], replicated
- d_gain_two: float32 [768], replicated
- d_shift_two: float32 [768], replicated
Inputs may be any that keep to these rules, and one draw needn't show every extreme that they name: `lengths`: every chain fills more than half of its 160 positions.
All inputs are finite; a program needn't handle non-finite values.
Results may differ from a plain program's by a relative error of at most 0.015.
Values may be sent and summed in bfloat16 or wider, within the bound.
No kernel may reach another device: no remote copies, remote signals or barrier semaphores. Data moves between devices by JAX's collectives and lax.ppermute only.
A program may use at most 256 MiB of HBM per device.

v0:
```python
import jax
import jax.numpy as jnp
from jax import lax
from jax.sharding import PartitionSpec as P

H = 12
EPS = 1e-12


def norm_forward(h, gain, shift):
    centre = h - jnp.mean(h, -1, keepdims=True)
    scale = lax.rsqrt(jnp.mean(centre * centre, -1, keepdims=True) + EPS)
    unit = centre * scale
    return (unit * gain + shift, unit, scale)


def norm_backward(grad, unit, scale, gain):
    d_gain = jnp.sum(grad * unit, 0)
    d_shift = jnp.sum(grad, 0)
    inner = grad * gain
    d_h = scale * (
        inner
        - jnp.mean(inner, -1, keepdims=True)
        - unit * jnp.mean(inner * unit, -1, keepdims=True)
    )
    return (d_h, d_gain, d_shift)


def over_rows(left, right):
    return lax.dot_general(
        left, right, (((0,), (0,)), ((), ())), preferred_element_type=jnp.float32
    )


def times_trans(left, weight):
    return lax.dot_general(
        left, weight, (((1,), (1,)), ((), ())), preferred_element_type=jnp.float32
    )


def attn_scores(query, keys, live_keys):
    seqs, count, width = query.shape
    total = keys.shape[1]
    size = width // H
    q_heads = query.reshape(seqs, count, H, size)
    k_heads = keys.reshape(seqs, total, H, size)
    scores = (
        jnp.einsum("bqhe,bkhe->bhqk", q_heads, k_heads, preferred_element_type=jnp.float32) * 0.125
    )
    return jnp.where(live_keys[:, None, None, :], scores, -1000000000.0)


def packed(grads, count):
    flat = jnp.concatenate([g.reshape(-1) for g in grads])
    extra = -flat.shape[0] % count
    return flat.reshape(count, -1)


def unpacked(flat, grads):
    flat = flat.reshape(-1)
    pieces = []
    start = 0
    for grad in grads:
        number = grad.size
        pieces.append(flat[start : start + number].reshape(grad.shape))
        start = start + number
    return tuple(pieces)


def body(
    chains_in,
    lengths,
    d_out,
    w_query,
    b_query,
    w_key,
    w_value,
    b_value,
    w_output,
    b_output,
    gain_one,
    shift_one,
    w_inner,
    b_inner,
    w_outer,
    b_outer,
    gain_two,
    shift_two,
):
    f32 = jnp.float32
    low_type = jnp.bfloat16
    seqs, length, width = chains_in.shape
    rows = seqs * length
    size = width // H
    parts = lax.axis_size("dp")
    count = lax.axis_size("dp") * lax.axis_size("seq")
    place = jnp.arange(length, dtype=jnp.int32)
    live_rows = place[None, :] < lengths[:, None]
    flat_x = chains_in.reshape(rows, width)
    query = (
        (jnp.dot(flat_x, w_query, preferred_element_type=f32) + b_query)
        .astype(low_type)
        .reshape(seqs, length, width)
    )
    keys = (
        jnp.dot(flat_x, w_key, preferred_element_type=f32)
        .astype(low_type)
        .reshape(seqs, length, width)
    )
    values = (
        (jnp.dot(flat_x, w_value, preferred_element_type=f32) + b_value)
        .astype(low_type)
        .reshape(seqs, length, width)
    )
    scores = attn_scores(query, keys, live_rows)
    top = jnp.max(scores, -1, keepdims=True)
    expo = jnp.exp(scores - top)
    summed = jnp.sum(expo, -1, keepdims=True)
    prob_b = (expo / summed).astype(low_type)
    lse = top + jnp.log(summed)
    v_heads = values.reshape(seqs, length, H, size)
    mixed = (
        jnp.einsum("bhqk,bkhe->bqhe", prob_b, v_heads, preferred_element_type=f32)
        .reshape(rows, width)
        .astype(low_type)
    )
    h_one = flat_x.astype(f32) + jnp.dot(mixed, w_output, preferred_element_type=f32) + b_output
    first, unit_one, scale_one = norm_forward(h_one, gain_one, shift_one)
    live_flat = live_rows.reshape(rows)
    fin = first.astype(low_type)
    pre = jnp.dot(fin, w_inner, preferred_element_type=f32) + b_inner
    hidden = jax.nn.gelu(pre, approximate=False).astype(low_type)
    ffn_home = (jnp.dot(hidden, w_outer, preferred_element_type=f32) + b_outer).astype(low_type)
    h_two = first + ffn_home.astype(f32)
    second, unit_two, scale_two = norm_forward(h_two, gain_two, shift_two)
    keep = live_flat[:, None].astype(f32)
    layer_out = (second * keep).astype(low_type).reshape(seqs, length, width)
    grad_out = d_out.reshape(rows, width).astype(f32) * keep
    d_h_two, d_gain_two, d_shift_two = norm_backward(grad_out, unit_two, scale_two, gain_two)
    d_ffn = d_h_two.astype(low_type)
    d_w_outer = over_rows(hidden, d_ffn)
    d_b_outer = jnp.sum(d_ffn.astype(f32), 0)
    d_hidden = times_trans(d_ffn, w_outer)
    gelu_pull = jax.vjp(lambda z: jax.nn.gelu(z, approximate=False), pre)[1]
    d_pre = gelu_pull(d_hidden)[0].astype(low_type)
    d_w_inner = over_rows(fin, d_pre)
    d_b_inner = jnp.sum(d_pre.astype(f32), 0)
    d_fin = times_trans(d_pre, w_inner).astype(low_type)
    d_home = d_fin
    d_first = d_h_two + d_home.astype(f32)
    ffn_grads = (d_w_inner, d_b_inner, d_w_outer, d_b_outer, d_gain_two, d_shift_two)
    d_h_one, d_gain_one, d_shift_one = norm_backward(d_first, unit_one, scale_one, gain_one)
    d_attn = d_h_one.astype(low_type)
    d_w_output = over_rows(mixed, d_attn)
    d_b_output = jnp.sum(d_attn.astype(f32), 0)
    d_mixed = times_trans(d_attn, w_output).astype(low_type).reshape(seqs, length, H, size)
    scores = attn_scores(query, keys, live_rows)
    prob = jnp.exp(scores - lse)
    prob_b = prob.astype(low_type)
    d_prob = jnp.einsum("bqhe,bkhe->bhqk", d_mixed, v_heads, preferred_element_type=f32)
    delta = jnp.sum(prob * d_prob, -1, keepdims=True)
    d_scores = (prob * (d_prob - delta)).astype(low_type)
    k_heads = keys.reshape(seqs, length, H, size)
    q_heads = query.reshape(seqs, length, H, size)
    d_query = (
        (jnp.einsum("bhqk,bkhe->bqhe", d_scores, k_heads, preferred_element_type=f32) * 0.125)
        .astype(low_type)
        .reshape(rows, width)
    )
    d_key = (
        (jnp.einsum("bhqk,bqhe->bkhe", d_scores, q_heads, preferred_element_type=f32) * 0.125)
        .astype(low_type)
        .reshape(rows, width)
    )
    d_value = (
        jnp.einsum("bhqk,bqhe->bkhe", prob_b, d_mixed, preferred_element_type=f32)
        .astype(low_type)
        .reshape(rows, width)
    )
    d_w_query = over_rows(flat_x, d_query)
    d_b_query = jnp.sum(d_query.astype(f32), 0)
    d_w_key = over_rows(flat_x, d_key)
    d_w_value = over_rows(flat_x, d_value)
    d_b_value = jnp.sum(d_value.astype(f32), 0)
    d_x = (
        d_h_one
        + times_trans(d_query, w_query)
        + times_trans(d_key, w_key)
        + times_trans(d_value, w_value)
    )
    d_x = d_x.reshape(seqs, length, width)
    attn_grads = (
        d_w_query,
        d_b_query,
        d_w_key,
        d_w_value,
        d_b_value,
        d_w_output,
        d_b_output,
        d_gain_one,
        d_shift_one,
    )
    local_grads = attn_grads + ffn_grads
    big = [g for g in local_grads if g.ndim == 2]
    small = [g for g in local_grads if g.ndim == 1]
    sums = lax.psum(jnp.concatenate(small), ("dp", "seq"))
    small_sums = unpacked(sums, small)
    big_sums = []
    for grad in big:
        part = lax.psum_scatter(
            grad.astype(low_type), ("dp", "seq"), scatter_dimension=0, tiled=True
        )
        big_sums.append(lax.all_gather(part, ("dp", "seq"), axis=0, tiled=True).astype(f32))
    every = []
    for grad in local_grads:
        every.append(big_sums.pop(0) if grad.ndim == 2 else small_sums[0])
        small_sums = small_sums if grad.ndim == 2 else small_sums[1:]
    return (
        layer_out,
        d_x,
        every[0],
        every[1],
        every[2],
        every[3],
        every[4],
        every[5],
        every[6],
        every[7],
        every[8],
        every[9],
        every[10],
        every[11],
        every[12],
        every[13],
        every[14],
    )


def solution(mesh):
    return jax.shard_map(
        body,
        mesh=mesh,
        in_specs=(
            P(("dp", "seq"), None, None),
            P(("dp", "seq")),
            P(("dp", "seq"), None, None),
            P(),
            P(),
            P(),
            P(),
            P(),
            P(),
            P(),
            P(),
            P(),
            P(),
            P(),
            P(),
            P(),
            P(),
            P(),
        ),
        out_specs=(
            P(("dp", "seq"), None, None),
            P(("dp", "seq"), None, None),
            P(),
            P(),
            P(),
            P(),
            P(),
            P(),
            P(),
            P(),
            P(),
            P(),
            P(),
            P(),
            P(),
            P(),
            P(),
        ),
        check_vma=False,
    )
```

profile of v0, /device:TPU:0, one launch (start us, length us, event | category | flops | bytes accessed | tf_op | source)
XLA Modules:
  0.0 1139.7 jit_solution(12008616428699110538)
XLA Ops:
  7.2 2.6 add_convert_fusion.3
  9.8 2.6 reshape.191
  12.5 4.6 copy.78
  19.6 2.6 reshape.192
  22.2 4.5 copy.76
  29.3 2.6 reshape.193
  31.9 3.5 copy.77
  35.4 3.6 fusion.12
  47.0 4.1 convert_element_type.174
  51.2 2.6 fusion.46
  55.6 23.9 %multiply_convert_fusion.1 = (bf16[640,3072]{1,0:T(8,128)(2,1)S(1)}, f32[640,3072]{1,0:T(8,128)}, f32[640,3072]{1,0:T(8,128)}) fusion(f32[3072]{0:T(1024)S(1)} %copy-done.22, bf16[768,3072]{1,0:T(8,128)(2,1)} %param.30, f32[640,768]{1,0:T(8,128)} %copy-done.8, f32[768]{0:T(1024)S(1)} %copy-done.26, f32[768]{0:T(1024)S(1)} %copy-done.19, ...), kind=kOutput, calls=%fused_computation.7 | convolution fusion | flops 3152117760 | bytes 26369024 | tf_op jit(solution)/shard_map/dot_general | solution.py:131
  79.5 7.2 fusion.47
  90.2 3.3 convert_reduce_fusion.3
  93.5 11.6 %convert_reduce_fusion = (f32[3072]{0:T(1024)S(1)}, bf16[640,3072]{1,0:T(8,128)(2,1)S(1)}) fusion(f32[640,3072]{1,0:T(8,128)} %get-tuple-element.64, bf16[3072,768]{1,0:T(8,128)(2,1)} %param.32, f32[640,768]{1,0:T(8,128)S(1)} %get-tuple-element.60, f32[640,3072]{1,0:T(8,128)} %get-tuple-element.80, f32[3072]{0:T(1024)S(1)} %copy-done.22), kind=kOutput, calls=%fused_computation.2 | convolution fusion | flops 3053810688 | bytes 26370048 | tf_op jit(solution)/shard_map/dot_general | solution.py:36
  105.2 3.8 multiply_reduce_fusion.2
  112.9 4.1 reshape.194
  117.0 4.6 copy.82
  121.6 7.5 multiply_reduce_fusion
  129.1 4.9 multiply_convert_fusion
  138.9 3.6 fusion.26
  145.1 3.5 fusion.25
  151.6 3.6 fusion.27
  157.8 5.5 convert_reduce_fusion.1
  166.5 3.6 fusion.28
  170.1 2.5 copy.104
  172.8 3.3 convolution_convert_fusion.2
  176.2 9.1 convolution_convert_fusion.1
  185.3 8.8 convolution_convert_fusion
  194.3 49.8 %reduce-scatter.19.cloned.1.call-done = bf16[24,768]{1,0:T(8,128)(2,1)} async-done(((bf16[768,768]{1,0:T(8,128)(2,1)}), bf16[24,768]{1,0:T(8,128)(2,1)}) %reduce-scatter.19.cloned.1.call-update) | async-done | bytes 36880 | tf_op jit(solution)/shard_map/reduce_scatter | solution.py:210
  244.2 100.9 %reduce-scatter.21.cloned.1.call-done = bf16[24,768]{1,0:T(8,128)(2,1)} async-done(((bf16[768,768]{1,0:T(8,128)(2,1)}), bf16[24,768]{1,0:T(8,128)(2,1)}) %reduce-scatter.21.cloned.1.call-update) | async-done | bytes 36880 | tf_op jit(solution)/shard_map/reduce_scatter | solution.py:210
  345.1 100.4 %reduce-scatter.23.cloned.1.call-done = bf16[24,768]{1,0:T(8,128)(2,1)} async-done(((bf16[768,768]{1,0:T(8,128)(2,1)}), bf16[24,768]{1,0:T(8,128)(2,1)}) %reduce-scatter.23.cloned.1.call-update) | async-done | bytes 36880 | tf_op jit(solution)/shard_map/reduce_scatter | solution.py:210
  445.6 100.8 %reduce-scatter.13.cloned.1.call-done = bf16[24,768]{1,0:T(8,128)(2,1)} async-done(((bf16[768,768]{1,0:T(8,128)(2,1)}), bf16[24,768]{1,0:T(8,128)(2,1)}) %reduce-scatter.13.cloned.1.call-update) | async-done | bytes 36880 | tf_op jit(solution)/shard_map/reduce_scatter | solution.py:210
  546.4 111.9 %reduce-scatter.15.cloned.1.call-done = bf16[24,3072]{1,0:T(8,128)(2,1)} async-done(((bf16[768,3072]{1,0:T(8,128)(2,1)}), bf16[24,3072]{1,0:T(8,128)(2,1)}) %reduce-scatter.15.cloned.1.call-update) | async-done | bytes 147472 | tf_op jit(solution)/shard_map/reduce_scatter | solution.py:210
  658.4 112.9 %reduce-scatter.17.cloned.1.call-done = bf16[96,768]{1,0:T(8,128)(2,1)} async-done(((bf16[3072,768]{1,0:T(8,128)(2,1)}), bf16[96,768]{1,0:T(8,128)(2,1)}) %reduce-scatter.17.cloned.1.call-update) | async-done | bytes 147472 | tf_op jit(solution)/shard_map/reduce_scatter | solution.py:210
  771.5 40.6 %psum.7 = f32[9216]{0:T(1024)S(1)} all-reduce(f32[9216]{0:T(1024)S(1)} %constant_dynamic-update-slice_fusion), channel_id=1, replica_groups=mesh['dp'=16,'seq'=2] {'dp','seq'}, use_global_device_ids=true, to_apply=%region_21.22 | all-reduce | flops 9216 | bytes 73728 | tf_op jit(solution)/shard_map/psum | solution.py:206
  813.4 2.7 fusion.49
  820.0 7.2 all-gather.7.cloned.1.call-done
  827.3 2.8 convert_element_type.202
  830.1 53.1 %all-gather.9.cloned.1.call-done = bf16[768,768]{1,0:T(8,128)(2,1)} async-done(((bf16[24,768]{1,0:T(8,128)(2,1)}), bf16[768,768]{1,0:T(8,128)(2,1)}) %all-gather.9.cloned.1.call-update) | async-done | bytes 1179664 | tf_op jit(solution)/shard_map/all_gather | solution.py:213
  883.2 2.8 convert_element_type.210
  886.0 53.1 %all-gather.11.cloned.1.call-done = bf16[768,768]{1,0:T(8,128)(2,1)} async-done(((bf16[24,768]{1,0:T(8,128)(2,1)}), bf16[768,768]{1,0:T(8,128)(2,1)}) %all-gather.11.cloned.1.call-update) | async-done | bytes 1179664 | tf_op jit(solution)/shard_map/all_gather | solution.py:213
  939.1 2.8 convert_element_type.213
  941.9 52.9 %all-gather.13.cloned.1.call-done = bf16[768,768]{1,0:T(8,128)(2,1)} async-done(((bf16[24,768]{1,0:T(8,128)(2,1)}), bf16[768,768]{1,0:T(8,128)(2,1)}) %all-gather.13.cloned.1.call-update) | async-done | bytes 1179664 | tf_op jit(solution)/shard_map/all_gather | solution.py:213
  994.8 2.8 convert_element_type.215
  997.7 62.7 %all-gather.15.cloned.1.call-done = bf16[768,3072]{1,0:T(8,128)(2,1)} async-done(((bf16[24,3072]{1,0:T(8,128)(2,1)}), bf16[768,3072]{1,0:T(8,128)(2,1)}) %all-gather.15.cloned.1.call-update) | async-done | bytes 4718608 | tf_op jit(solution)/shard_map/all_gather | solution.py:213
  1060.4 7.4 convert_element_type.217
  1067.7 57.9 %all-gather.17.cloned.1.call-done = bf16[3072,768]{1,0:T(8,128)(2,1)} async-done(((bf16[96,768]{1,0:T(8,128)(2,1)}), bf16[3072,768]{1,0:T(8,128)(2,1)}) %all-gather.17.cloned.1.call-update) | async-done | bytes 4718608 | tf_op jit(solution)/shard_map/all_gather | solution.py:213
  1125.6 6.8 convert_element_type.219
  (134 shorter events, 44.2 us)
Async XLA Ops:
  7.2 43.9 %copy-start = (bf16[768,768]{1,0:T(8,128)(2,1)S(1)}, bf16[768,768]{1,0:T(8,128)(2,1)}, u32[]{:S(2)}) copy-start(bf16[768,768]{1,0:T(8,128)(2,1)} %param.26) | copy-start | bytes 3538948
  7.2 236.9 %reduce-scatter.19.cloned.1.call-start = ((), (), s32[]{:S(2)}) async-start(), calls=%async_computation.15 | async-start | bytes 1216512 | tf_op jit(solution)/shard_map/reduce_scatter | solution.py:210
  12.5 4.6 copy-start.20
  12.5 4.6 copy-start.23
  39.0 3.2 copy-start.1
  39.0 3.2 copy-start.11
  44.6 6.5 copy-start.24
  51.1 4.4 copy-start.19
  51.1 4.4 copy-start.22
  51.1 4.4 copy-start.26
  53.8 1.3 copy-start.8
  55.5 24.0 %copy-start.9 = (f32[640,768]{1,0:T(8,128)S(1)}, f32[640,768]{1,0:T(8,128)}, u32[]{:S(2)}) copy-start(f32[640,768]{1,0:T(8,128)} %copy-done.8) | copy-start | bytes 5898244
  55.5 24.0 %copy-start.25 = (f32[768]{0:T(1024)S(1)}, f32[768]{0:T(1024)}, u32[]{:S(2)}) copy-start(f32[768]{0:T(1024)} %param.33) | copy-start | bytes 9220
  79.5 7.2 copy-start.27
  79.5 7.6 copy-start.17
  86.7 3.3 copy-start.3
  86.7 1.9 copy-start.5
  87.1 3.0 copy-start.18
  90.2 15.0 %slice-start = ((s8[4718592]{0:T(1024)(128)(4,1)}), s8[4194304]{0:T(1024)(128)(4,1)S(1)}, s32[]{:S(2)}) async-start(s8[4718592]{0:T(1024)(128)(4,1)} %bitcast.81), calls=%async_computation.18 | async-start | bytes 8388608
  93.5 11.7 %copy-start.14 = (f32[640,768]{1,0:T(8,128)}, f32[640,768]{1,0:T(8,128)S(1)}, u32[]{:S(2)}) copy-start(f32[640,768]{1,0:T(8,128)S(1)} %get-tuple-element.60) | copy-start | bytes 5898244
  93.5 11.7 %copy-start.10 = (f32[640,768]{1,0:T(8,128)S(1)}, f32[640,768]{1,0:T(8,128)}, u32[]{:S(2)}) copy-start(f32[640,768]{1,0:T(8,128)} %copy-done.8) | copy-start | bytes 5898244
  93.5 11.7 %slice-start.1 = ((s8[4718592]{0:T(1024)(128)(4,1)}), s8[524288]{0:T(1024)(128)(4,1)S(1)}, s32[]{:S(2)}) async-start(s8[4718592]{0:T(1024)(128)(4,1)} %bitcast.81), calls=%async_computation.19 | async-start | bytes 1048576
  105.1 3.9 copy-start.28
  109.7 1.3 copy-start.6
  134.0 1.9 copy-start.2
  142.5 2.6 copy-start.4
  145.0 200.0 %reduce-scatter.21.cloned.1.call-start = ((), (), s32[]{:S(2)}) async-start(), calls=%async_computation.16 | async-start | bytes 1216512 | tf_op jit(solution)/shard_map/reduce_scatter | solution.py:210
  155.2 2.6 copy-start.12
  157.7 287.8 %reduce-scatter.23.cloned.1.call-start = ((), (), s32[]{:S(2)}) async-start(), calls=%async_computation.17 | async-start | bytes 1216512 | tf_op jit(solution)/shard_map/reduce_scatter | solution.py:210
  170.1 2.6 copy-start.7
  172.7 373.6 %reduce-scatter.13.cloned.1.call-start = ((), (), s32[]{:S(2)}) async-start(), calls=%async_computation.9 | async-start | bytes 1216512 | tf_op jit(solution)/shard_map/reduce_scatter | solution.py:210
  176.1 482.2 %reduce-scatter.15.cloned.1.call-start = ((), (), s32[]{:S(2)}) async-start(), calls=%async_computation.11 | async-start | bytes 4866048 | tf_op jit(solution)/shard_map/reduce_scatter | solution.py:210
  185.3 585.9 %reduce-scatter.17.cloned.1.call-start = ((), (), s32[]{:S(2)}) async-start(), calls=%async_computation.13 | async-start | bytes 4866048 | tf_op jit(solution)/shard_map/reduce_scatter | solution.py:210
  194.2 633.1 %all-gather.7.cloned.1.call-start = ((), (), s32[]{:S(2)}) async-start(), calls=%async_computation.6 | async-start | bytes 1216512 | tf_op jit(solution)/shard_map/all_gather | solution.py:213
  244.1 639.1 %all-gather.9.cloned.1.call-start = ((), (), s32[]{:S(2)}) async-start(), calls=%async_computation.7 | async-start | bytes 1216512 | tf_op jit(solution)/shard_map/all_gather | solution.py:213
  345.0 594.0 %all-gather.11.cloned.1.call-start = ((), (), s32[]{:S(2)}) async-start(), calls=%async_computation.8 | async-start | bytes 1216512 | tf_op jit(solution)/shard_map/all_gather | solution.py:213
  445.5 549.3 %all-gather.13.cloned.1.call-start = ((), (), s32[]{:S(2)}) async-start(), calls=%async_computation.10 | async-start | bytes 1216512 | tf_op jit(solution)/shard_map/all_gather | solution.py:213
  546.3 514.0 %all-gather.15.cloned.1.call-start = ((), (), s32[]{:S(2)}) async-start(), calls=%async_computation.12 | async-start | bytes 4866048 | tf_op jit(solution)/shard_map/all_gather | solution.py:213
  658.3 467.3 %all-gather.17.cloned.1.call-start = ((), (), s32[]{:S(2)}) async-start(), calls=%async_computation.14 | async-start | bytes 4866048 | tf_op jit(solution)/shard_map/all_gather | solution.py:213
  812.7 3.4 copy-start.16
  812.7 3.4 copy-start.21
  816.1 1.2 copy-start.13
  816.1 1.6 copy-start.15
Sparse Core Ops, SparseCore 0:
  145.2 98.8 reduce-scatter.18
  249.7 95.2 reduce-scatter.20
  350.1 95.3 reduce-scatter.22
  451.0 95.2 reduce-scatter.12
  552.2 106.0 reduce-scatter.14
  665.1 106.0 reduce-scatter.16
  774.1 53.1 all-gather.6
  830.2 52.9 all-gather.8
  886.1 52.9 all-gather.10
  941.8 52.9 all-gather.12
  997.7 62.5 all-gather.14
  1063.1 62.4 all-gather.16
where the time goes:
time: 1150 us; the launch traced here: 1140 us
  waiting for transfers between devices  864 us (75%)
  matrix products  120 us (10%)
  local copies, waits for them, and re-layouts  60.8 us (5%)
  blocking collectives  40.6 us (4%)
  other arithmetic  38.7 us (3%)
  between operations  15.3 us (1%)
    reduce_scatter x6, waiting for transfers between devices, body(): lax.psum_scatter(grad.astype(low_type), ('dp', 'seq'), scatter_dimension=...  577 us
    all_gather x6, waiting for transfers between devices, body(): lax.all_gather(part, ('dp', 'seq'), axis=0, tiled=True).astype(f32)  287 us
    psum x1, blocking collectives, body(): sums = lax.psum(jnp.concatenate(small), ('dp', 'seq'))  40.6 us
    dot_general x6, matrix products, over_rows(): lax.dot_general(left, right, (((0,), (0,)), ((), ())), preferred_element_...  32.1 us
    convert_element_type x6, other arithmetic, body(): lax.all_gather(part, ('dp', 'seq'), axis=0, tiled=True).astype(f32)  25.6 us
    dot_general x1, matrix products, body(): pre = jnp.dot(fin, w_inner, preferred_element_type=f32) + b_inner  23.9 us
    dot_general x6, matrix products, times_trans(): lax.dot_general(left, weight, (((1,), (1,)), ((), ())), preferred_element...  23.5 us
  transfers between devices with their start and end apart: 12, of which 12 were waited for; matrix products, arithmetic and copies ran while one was open for 7% of the time, Pallas kernels for 0%

commit v1 on v0

--- a/solution.py
+++ b/solution.py
@@ -203,7 +203,7 @@
     local_grads = attn_grads + ffn_grads
     big = [g for g in local_grads if g.ndim == 2]
     small = [g for g in local_grads if g.ndim == 1]
-    sums = lax.psum(jnp.concatenate(small), ("dp", "seq"))
+    sums = jnp.sum(lax.all_gather(jnp.concatenate(small), ("dp", "seq")), axis=0)
     small_sums = unpacked(sums, small)
     big_sums = []
     for grad in big:

time: 1150 us -> 1210 us (1.052)
  waiting for transfers between devices: 864 us -> 958 us
  blocking collectives: 40.6 us -> 0 us
    all_gather x0 -> x1, waiting for transfers between devices: none -> 50 us  [body(): lax.all_gather(jnp.concatenate(small), ('dp', 'seq'))]
    all_gather x6, waiting for transfers between devices: 287 us -> 333 us  [body(): lax.all_gather(part, ('dp', 'seq'), axis=0, tiled=True).astype(f32)]
    psum x1 -> x0, blocking collectives: 40.6 us -> none  [body(): sums = lax.psum(jnp.concatenate(small), ('dp', 'seq'))]
  transfers between devices with their start and end apart: 12 -> 13, of which waited for: 12 -> 13; matrix products, arithmetic and copies ran while one was open for 7% -> 6% of each run, Pallas kernels for 0% -> 0%
where the time goes in v1:
time: 1210 us; the launch traced here: 1200 us
  waiting for transfers between devices  958 us (79%)
  matrix products  120 us (10%)
  local copies, waits for them, and re-layouts  62.8 us (5%)
  other arithmetic  38.8 us (3%)
  between operations  15 us (1%)
    reduce_scatter x6, waiting for transfers between devices, body(): lax.psum_scatter(grad.astype(low_type), ('dp', 'seq'), scatter_dimension=...  575 us
    all_gather x6, waiting for transfers between devices, body(): lax.all_gather(part, ('dp', 'seq'), axis=0, tiled=True).astype(f32)  333 us
    all_gather x1, waiting for transfers between devices, body(): lax.all_gather(jnp.concatenate(small), ('dp', 'seq'))  50 us
    dot_general x6, matrix products, over_rows(): lax.dot_general(left, right, (((0,), (0,)), ((), ())), preferred_element_...  32.1 us
    convert_element_type x6, other arithmetic, body(): lax.all_gather(part, ('dp', 'seq'), axis=0, tiled=True).astype(f32)  25.6 us
  transfers between devices with their start and end apart: 13, of which 13 were waited for; matrix products, arithmetic and copies ran while one was open for 6% of the time, Pallas kernels for 0%

profile of v1, /device:TPU:0, one launch (start us, length us, event | category | flops | bytes accessed | tf_op | source)
XLA Modules:
  0.0 1195.8 jit_solution(10338582150074028869)
XLA Ops:
  7.2 2.6 add_convert_fusion.3
  9.8 2.6 reshape.192
  12.5 4.6 copy.101
  19.6 2.6 reshape.193
  22.2 4.5 copy.99
  29.3 2.6 reshape.194
  31.9 3.5 copy.100
  35.4 3.6 fusion.12
  47.0 4.1 convert_element_type.174
  51.1 2.6 fusion.46
  55.5 23.9 %multiply_convert_fusion.1 = (bf16[640,3072]{1,0:T(8,128)(2,1)S(1)}, f32[640,3072]{1,0:T(8,128)}, f32[640,3072]{1,0:T(8,128)}) fusion(f32[3072]{0:T(1024)S(1)} %copy-done.23, bf16[768,3072]{1,0:T(8,128)(2,1)} %param.30, f32[640,768]{1,0:T(8,128)} %copy-done.8, f32[768]{0:T(1024)S(1)} %copy-done.27, f32[768]{0:T(1024)S(1)} %copy-done.20, ...), kind=kOutput, calls=%fused_computation.7 | convolution fusion | flops 3152117760 | bytes 26369024 | tf_op jit(solution)/shard_map/dot_general | solution.py:131
  79.5 7.2 fusion.47
  90.2 3.3 convert_reduce_fusion.3
  93.5 11.6 convert_reduce_fusion
  105.2 3.8 multiply_reduce_fusion.2
  112.9 4.1 reshape.195
  117.0 4.5 copy.105
  121.5 7.5 multiply_reduce_fusion
  129.0 4.9 multiply_convert_fusion
  138.8 3.6 fusion.26
  145.1 3.5 fusion.25
  151.5 3.6 fusion.27
  157.7 5.5 convert_reduce_fusion.1
  166.5 3.6 fusion.28
  170.1 2.6 copy.127
  172.7 3.3 convolution_convert_fusion.2
  176.1 9.1 convolution_convert_fusion.1
  185.3 8.8 convolution_convert_fusion
  195.1 48.9 %reduce-scatter.19.cloned.1.call-done = bf16[24,768]{1,0:T(8,128)(2,1)} async-done(((bf16[768,768]{1,0:T(8,128)(2,1)}), bf16[24,768]{1,0:T(8,128)(2,1)}) %reduce-scatter.19.cloned.1.call-update) | async-done | bytes 36880 | tf_op jit(solution)/shard_map/reduce_scatter | solution.py:210
  244.1 100.9 %reduce-scatter.21.cloned.1.call-done = bf16[24,768]{1,0:T(8,128)(2,1)} async-done(((bf16[768,768]{1,0:T(8,128)(2,1)}), bf16[24,768]{1,0:T(8,128)(2,1)}) %reduce-scatter.21.cloned.1.call-update) | async-done | bytes 36880 | tf_op jit(solution)/shard_map/reduce_scatter | solution.py:210
  345.1 100.4 %reduce-scatter.23.cloned.1.call-done = bf16[24,768]{1,0:T(8,128)(2,1)} async-done(((bf16[768,768]{1,0:T(8,128)(2,1)}), bf16[24,768]{1,0:T(8,128)(2,1)}) %reduce-scatter.23.cloned.1.call-update) | async-done | bytes 36880 | tf_op jit(solution)/shard_map/reduce_scatter | solution.py:210
  445.5 100.8 %reduce-scatter.13.cloned.1.call-done = bf16[24,768]{1,0:T(8,128)(2,1)} async-done(((bf16[768,768]{1,0:T(8,128)(2,1)}), bf16[24,768]{1,0:T(8,128)(2,1)}) %reduce-scatter.13.cloned.1.call-update) | async-done | bytes 36880 | tf_op jit(solution)/shard_map/reduce_scatter | solution.py:210
  546.3 111.8 %reduce-scatter.15.cloned.1.call-done = bf16[24,3072]{1,0:T(8,128)(2,1)} async-done(((bf16[768,3072]{1,0:T(8,128)(2,1)}), bf16[24,3072]{1,0:T(8,128)(2,1)}) %reduce-scatter.15.cloned.1.call-update) | async-done | bytes 147472 | tf_op jit(solution)/shard_map/reduce_scatter | solution.py:210
  658.5 112.7 %reduce-scatter.17.cloned.1.call-done = bf16[96,768]{1,0:T(8,128)(2,1)} async-done(((bf16[3072,768]{1,0:T(8,128)(2,1)}), bf16[96,768]{1,0:T(8,128)(2,1)}) %reduce-scatter.17.cloned.1.call-update) | async-done | bytes 147472 | tf_op jit(solution)/shard_map/reduce_scatter | solution.py:210
  771.2 2.7 fusion.49
  777.8 50.0 %all-gather.21.cloned.1.call-done = f32[294912]{0:T(1024)} async-done(((f32[9216]{0:T(1024)}), f32[294912]{0:T(1024)}) %all-gather.21.cloned.1.call-update) | async-done | bytes 1179664 | tf_op jit(solution)/shard_map/all_gather | solution.py:206
  830.6 53.1 %all-gather.9.cloned.1.call-done = bf16[768,768]{1,0:T(8,128)(2,1)} async-done(((bf16[24,768]{1,0:T(8,128)(2,1)}), bf16[768,768]{1,0:T(8,128)(2,1)}) %all-gather.9.cloned.1.call-update) | async-done | bytes 1179664 | tf_op jit(solution)/shard_map/all_gather | solution.py:213
  883.7 2.8 convert_element_type.202
  886.6 53.1 %all-gather.11.cloned.1.call-done = bf16[768,768]{1,0:T(8,128)(2,1)} async-done(((bf16[24,768]{1,0:T(8,128)(2,1)}), bf16[768,768]{1,0:T(8,128)(2,1)}) %all-gather.11.cloned.1.call-update) | async-done | bytes 1179664 | tf_op jit(solution)/shard_map/all_gather | solution.py:213
  939.6 2.8 convert_element_type.210
  942.5 52.9 %all-gather.13.cloned.1.call-done = bf16[768,768]{1,0:T(8,128)(2,1)} async-done(((bf16[24,768]{1,0:T(8,128)(2,1)}), bf16[768,768]{1,0:T(8,128)(2,1)}) %all-gather.13.cloned.1.call-update) | async-done | bytes 1179664 | tf_op jit(solution)/shard_map/all_gather | solution.py:213
  995.4 2.8 convert_element_type.213
  998.2 53.1 %all-gather.15.cloned.1.call-done = bf16[768,768]{1,0:T(8,128)(2,1)} async-done(((bf16[24,768]{1,0:T(8,128)(2,1)}), bf16[768,768]{1,0:T(8,128)(2,1)}) %all-gather.15.cloned.1.call-update) | async-done | bytes 1179664 | tf_op jit(solution)/shard_map/all_gather | solution.py:213
  1051.3 2.8 convert_element_type.215
  1054.1 62.5 %all-gather.17.cloned.1.call-done = bf16[768,3072]{1,0:T(8,128)(2,1)} async-done(((bf16[24,3072]{1,0:T(8,128)(2,1)}), bf16[768,3072]{1,0:T(8,128)(2,1)}) %all-gather.17.cloned.1.call-update) | async-done | bytes 4718608 | tf_op jit(solution)/shard_map/all_gather | solution.py:213
  1116.7 7.4 convert_element_type.217
  1124.0 58.0 %all-gather.19.cloned.1.call-done = bf16[3072,768]{1,0:T(8,128)(2,1)} async-done(((bf16[96,768]{1,0:T(8,128)(2,1)}), bf16[3072,768]{1,0:T(8,128)(2,1)}) %all-gather.19.cloned.1.call-update) | async-done | bytes 4718608 | tf_op jit(solution)/shard_map/all_gather | solution.py:213
  1182.0 6.8 convert_element_type.219
  (140 shorter events, 46.7 us)
Async XLA Ops:
  7.2 43.9 %copy-start = (bf16[768,768]{1,0:T(8,128)(2,1)S(1)}, bf16[768,768]{1,0:T(8,128)(2,1)}, u32[]{:S(2)}) copy-start(bf16[768,768]{1,0:T(8,128)(2,1)} %param.26) | copy-start | bytes 3538948
  7.2 236.8 %reduce-scatter.19.cloned.1.call-start = ((), (), s32[]{:S(2)}) async-start(), calls=%async_computation.16 | async-start | bytes 1216512 | tf_op jit(solution)/shard_map/reduce_scatter | solution.py:210
  12.5 4.6 copy-start.21
  12.5 4.6 copy-start.24
  39.0 3.2 copy-start.1
  39.0 3.2 copy-start.11
  44.6 6.5 copy-start.25
  51.1 4.4 copy-start.20
  51.1 4.4 copy-start.23
  51.1 4.4 copy-start.27
  53.8 1.3 copy-start.8
  55.5 24.0 %copy-start.9 = (f32[640,768]{1,0:T(8,128)S(1)}, f32[640,768]{1,0:T(8,128)}, u32[]{:S(2)}) copy-start(f32[640,768]{1,0:T(8,128)} %copy-done.8) | copy-start | bytes 5898244
  55.5 24.0 %copy-start.26 = (f32[768]{0:T(1024)S(1)}, f32[768]{0:T(1024)}, u32[]{:S(2)}) copy-start(f32[768]{0:T(1024)} %param.33) | copy-start | bytes 9220
  79.5 7.2 copy-start.28
  79.5 7.6 copy-start.18
  86.7 3.3 copy-start.3
  86.7 1.9 copy-start.5
  87.1 3.0 copy-start.19
  90.1 15.0 %slice-start = ((s8[4718592]{0:T(1024)(128)(4,1)}), s8[4194304]{0:T(1024)(128)(4,1)S(1)}, s32[]{:S(2)}) async-start(s8[4718592]{0:T(1024)(128)(4,1)} %bitcast.81), calls=%async_computation.19 | async-start | bytes 8388608
  93.5 11.7 copy-start.14
  93.5 11.7 copy-start.10
  93.5 11.7 slice-start.1
  105.1 3.9 copy-start.29
  109.6 1.3 copy-start.6
  133.9 1.9 copy-start.2
  142.4 2.6 copy-start.4
  145.0 200.0 %reduce-scatter.21.cloned.1.call-start = ((), (), s32[]{:S(2)}) async-start(), calls=%async_computation.17 | async-start | bytes 1216512 | tf_op jit(solution)/shard_map/reduce_scatter | solution.py:210
  155.1 2.6 copy-start.12
  157.7 287.8 %reduce-scatter.23.cloned.1.call-start = ((), (), s32[]{:S(2)}) async-start(), calls=%async_computation.18 | async-start | bytes 1216512 | tf_op jit(solution)/shard_map/reduce_scatter | solution.py:210
  170.1 2.6 copy-start.7
  172.7 373.6 %reduce-scatter.13.cloned.1.call-start = ((), (), s32[]{:S(2)}) async-start(), calls=%async_computation.9 | async-start | bytes 1216512 | tf_op jit(solution)/shard_map/reduce_scatter | solution.py:210
  176.1 482.1 %reduce-scatter.15.cloned.1.call-start = ((), (), s32[]{:S(2)}) async-start(), calls=%async_computation.11 | async-start | bytes 4866048 | tf_op jit(solution)/shard_map/reduce_scatter | solution.py:210
  185.2 585.9 %reduce-scatter.17.cloned.1.call-start = ((), (), s32[]{:S(2)}) async-start(), calls=%async_computation.13 | async-start | bytes 4866048 | tf_op jit(solution)/shard_map/reduce_scatter | solution.py:210
  194.1 633.7 %all-gather.21.cloned.1.call-start = ((), (), s32[]{:S(2)}) async-start(), calls=%async_computation.15 | async-start | bytes 1216512 | tf_op jit(solution)/shard_map/all_gather | solution.py:206
  194.4 0.6 copy-start.17
  195.1 688.6 %all-gather.9.cloned.1.call-start = ((), (), s32[]{:S(2)}) async-start(), calls=%async_computation.6 | async-start | bytes 1216512 | tf_op jit(solution)/shard_map/all_gather | solution.py:213
  244.1 695.6 %all-gather.11.cloned.1.call-start = ((), (), s32[]{:S(2)}) async-start(), calls=%async_computation.7 | async-start | bytes 1216512 | tf_op jit(solution)/shard_map/all_gather | solution.py:213
  345.0 650.4 %all-gather.13.cloned.1.call-start = ((), (), s32[]{:S(2)}) async-start(), calls=%async_computation.8 | async-start | bytes 1216512 | tf_op jit(solution)/shard_map/all_gather | solution.py:213
  445.5 605.8 %all-gather.15.cloned.1.call-start = ((), (), s32[]{:S(2)}) async-start(), calls=%async_computation.10 | async-start | bytes 1216512 | tf_op jit(solution)/shard_map/all_gather | solution.py:213
  546.3 570.4 %all-gather.17.cloned.1.call-start = ((), (), s32[]{:S(2)}) async-start(), calls=%async_computation.12 | async-start | bytes 4866048 | tf_op jit(solution)/shard_map/all_gather | solution.py:213
  658.2 523.8 %all-gather.19.cloned.1.call-start = ((), (), s32[]{:S(2)}) async-start(), calls=%async_computation.14 | async-start | bytes 4866048 | tf_op jit(solution)/shard_map/all_gather | solution.py:213
  771.2 2.7 copy-start.16
  771.2 2.7 copy-start.22
  773.9 1.2 copy-start.13
  773.9 1.6 copy-start.15
Sparse Core Ops, SparseCore 0:
  145.1 98.8 reduce-scatter.18
  249.7 95.2 reduce-scatter.20
  350.1 95.2 reduce-scatter.22
  450.9 95.2 reduce-scatter.12
  552.2 105.9 reduce-scatter.14
  665.0 106.1 reduce-scatter.16
  774.6 53.1 all-gather.20
  830.7 52.9 all-gather.8
  886.6 52.9 all-gather.10
  942.4 52.9 all-gather.12
  998.3 52.9 all-gather.14
  1054.0 62.5 all-gather.16
  1119.5 62.4 all-gather.18
